TPU v7x, 32 devices: a whole 2x2x4 slice. The times are simulated.
32 devices in a mesh: dp: 4 (over z), blk: 4 (over y, core), aa: 2 (over x).
Axes of the slice: x: 2, y: 2, z: 4, core: 2. Of those that a mesh axis runs over, the one named last changes fastest.
Arguments:
- queries: bfloat16 [4, 1024, 2048], P('dp', ('blk', 'aa')), may hold values from -128 to 128
- keys: bfloat16 [4, 1024, 512], P('dp', ('blk', 'aa')), may hold values from -10 to 10
- values: bfloat16 [4, 1024, 512], P('dp', ('blk', 'aa')), may hold values from -6 to 6
- grad_parts: float32 [4, 8, 131072], P('dp', ('blk', 'aa')), may hold values from -192 to 192
Outputs:
- attended: bfloat16 [4, 1024, 2048], P('dp', 'blk', 'aa')
- grad_mean: float32 [131072], P(('blk', 'aa'))
All inputs are finite; a program needn't handle non-finite values.
Results may differ from a plain program's by a relative error of at most 0.008.
Values may be sent and summed in bfloat16 or wider, within the bound.
A program may use at most 64 MiB of HBM per device.

v0:
```python
import jax
import jax.numpy as jnp
from jax import lax
from jax.sharding import PartitionSpec as P

HQ = 16
KVH = 4
DH = 128


def shifted(value, axis, by):
    peers = lax.axis_size(axis)
    pairs = [(i, i + by) for i in range(peers) if 0 <= i + by < peers]
    return lax.ppermute(value, axis, pairs)


def attend(queries, keys, values):
    rows = queries.shape[0]
    size_aa = lax.axis_size("aa")
    spread = max(KVH, size_aa)
    q_heads = queries.reshape(rows, HQ, DH)
    k_heads = jnp.repeat(keys.reshape(rows, KVH, DH), spread // KVH, axis=1)
    v_heads = jnp.repeat(values.reshape(rows, KVH, DH), spread // KVH, axis=1)
    q_here, k_here, v_here = (
        lax.all_to_all(q_heads, "aa", split_axis=1, concat_axis=0, tiled=True),
        lax.all_to_all(k_heads, "aa", split_axis=1, concat_axis=0, tiled=True),
        lax.all_to_all(v_heads, "aa", split_axis=1, concat_axis=0, tiled=True),
    )
    span = q_here.shape[0]
    reach = span // 4
    prior_k, prior_v = shifted((k_here[span - reach :], v_here[span - reach :]), "blk", 1)
    group = q_here.shape[1] // k_here.shape[1]
    k_all = jnp.repeat(jnp.concatenate([prior_k, k_here], 0), group, axis=1)
    v_all = jnp.repeat(jnp.concatenate([prior_v, v_here], 0), group, axis=1)
    step_rows = min(256, reach)
    anchor = lax.axis_index("blk") * span
    scale = DH ** (-0.5)

    def one_block(index):
        offset = index * step_rows
        q_block = lax.dynamic_slice_in_dim(q_here, offset, step_rows, 0)
        k_block = lax.dynamic_slice_in_dim(k_all, offset, step_rows + reach, 0)
        v_block = lax.dynamic_slice_in_dim(v_all, offset, step_rows + reach, 0)
        scores = (
            jnp.einsum("qhd,khd->hqk", q_block, k_block, preferred_element_type=jnp.float32) * scale
        )
        q_pos = anchor + offset + jnp.arange(step_rows, dtype=jnp.int32)
        k_pos = anchor + offset - reach + jnp.arange(step_rows + reach, dtype=jnp.int32)
        allowed = (k_pos[None, :] <= q_pos[:, None]) & (k_pos[None, :] > q_pos[:, None] - reach)
        scores = jnp.where(allowed[None], scores, -1e30)
        top = jnp.max(scores, axis=-1, keepdims=True)
        expo = jnp.exp(scores - top)
        weights = (expo / jnp.sum(expo, axis=-1, keepdims=True)).astype(jnp.bfloat16)
        out = jnp.einsum("hqk,khd->qhd", weights, v_block, preferred_element_type=jnp.float32)
        return out.astype(jnp.bfloat16)

    blocks = lax.map(one_block, jnp.arange(span // step_rows, dtype=jnp.int32))
    return blocks.reshape(span, -1)


def average(grad_parts):
    members = lax.axis_size("blk") * lax.axis_size("aa")
    replicas = lax.axis_size("dp")
    flat_grad = grad_parts.reshape(-1)
    share = lax.psum_scatter(flat_grad, ("blk", "aa"), scatter_dimension=0, tiled=True)
    total = lax.psum(share, "dp")
    return total / (members * replicas)


def shards(queries, keys, values, grad_parts):
    attended = attend(queries[0], keys[0], values[0])[None]
    grad_mean = average(grad_parts)
    return (attended, grad_mean)


def solution(mesh):
    placed = (
        P("dp", ("blk", "aa"), None),
        P("dp", ("blk", "aa"), None),
        P("dp", ("blk", "aa"), None),
        P("dp", ("blk", "aa"), None),
    )
    return jax.shard_map(
        shards,
        mesh=mesh,
        in_specs=placed,
        out_specs=(P("dp", "blk", "aa"), P(("blk", "aa"))),
        check_vma=False,
    )
```

profile of v0, /device:TPU:0, one launch (start us, length us, event | category | flops | bytes accessed | tf_op | source)
XLA Modules:
  0.0 135.1 jit_solution(9205147777204657953)
XLA Ops:
  7.2 1.0 copy.38
  8.2 0.8 copy.39
  9.0 4.4 %all-to-all-start.2 = ((bf16[128,4,128]{2,0,1:T(8,128)(2,1)}), bf16[128,4,128]{2,0,1:T(8,128)(2,1)S(1)}, u32[]{:S(2)}, u32[]{:S(2)}) async-start(bf16[128,4,128]{2,0,1:T(8,128)(2,1)} %copy.39), calls=%async_computation.2 | async-start | bytes 262144 | tf_op jit(solution)/shard_map/all_to_all | solution.py:26
  13.3 0.1 copy.31
  13.5 0.8 copy.32
  14.2 3.7 %all-to-all-done.2 = bf16[128,4,128]{2,0,1:T(8,128)(2,1)S(1)} async-done(((bf16[128,4,128]{2,0,1:T(8,128)(2,1)}), bf16[128,4,128]{2,0,1:T(8,128)(2,1)S(1)}, u32[]{:S(2)}, u32[]{:S(2)}) %all-to-all-start.2) | async-done | bytes 131104 | tf_op jit(solution)/shard_map/all_to_all | solution.py:26
  17.9 3.4 %all-to-all-start = ((bf16[128,4,128]{2,0,1:T(8,128)(2,1)}), bf16[128,4,128]{2,0,1:T(8,128)(2,1)S(1)}, u32[]{:S(2)}, u32[]{:S(2)}) async-start(bf16[128,4,128]{2,0,1:T(8,128)(2,1)} %copy.32), calls=%async_computation | async-start | bytes 262144 | tf_op jit(solution)/shard_map/all_to_all | solution.py:27
  21.3 1.3 collective-permute-start.1
  22.6 0.3 copy.34
  22.9 1.0 copy.35
  23.9 1.8 %all-to-all-done = bf16[128,4,128]{2,0,1:T(8,128)(2,1)S(1)} async-done(((bf16[128,4,128]{2,0,1:T(8,128)(2,1)}), bf16[128,4,128]{2,0,1:T(8,128)(2,1)S(1)}, u32[]{:S(2)}, u32[]{:S(2)}) %all-to-all-start) | async-done | bytes 131104 | tf_op jit(solution)/shard_map/all_to_all | solution.py:27
  25.7 3.5 %all-to-all-start.1 = ((bf16[128,16,128]{2,0,1:T(8,128)(2,1)}), bf16[128,16,128]{2,0,1:T(8,128)(2,1)S(1)}, u32[]{:S(2)}, u32[]{:S(2)}) async-start(bf16[128,16,128]{2,0,1:T(8,128)(2,1)} %copy.35), calls=%async_computation.1 | async-start | bytes 1048576 | tf_op jit(solution)/shard_map/all_to_all | solution.py:25
  29.2 0.0 all-reduce.6.cloned.1.call-start
  29.3 0.7 all-reduce.6.cloned.1.call-update
  30.0 0.6 copy-done.2
  30.7 0.6 dynamic-slice
  32.0 2.9 %collective-permute-start = (bf16[64,2,128]{2,0,1:T(8,128)(2,1)S(1)}, bf16[64,2,128]{2,0,1:T(8,128)(2,1)S(1)}, u32[]{:S(2)}, u32[]{:S(2)}) collective-permute-start(bf16[64,2,128]{2,0,1:T(8,128)(2,1)S(1)} %slice.8), channel_id=1, source_target_pairs={{0,2},{2,4},{4,6},{1,3},{3,5},{5,7},{8,10},{10,12},{12,14},{9,11},... | collective-permute-start | bytes 98312 | tf_op jit(solution)/shard_map/ppermute | solution.py:14
  34.9 0.8 collective-permute-done
  35.7 2.7 %all-to-all-done.1 = bf16[128,16,128]{2,0,1:T(8,128)(2,1)S(1)} async-done(((bf16[128,16,128]{2,0,1:T(8,128)(2,1)}), bf16[128,16,128]{2,0,1:T(8,128)(2,1)S(1)}, u32[]{:S(2)}, u32[]{:S(2)}) %all-to-all-start.1) | async-done | bytes 524320 | tf_op jit(solution)/shard_map/all_to_all | solution.py:25
  38.4 0.3 copy.37
  38.7 51.6 %all-reduce.6.cloned.1.call-done = f32[131072]{0:T(1024)} async-done(((f32[131072]{0:T(1024)}), f32[131072]{0:T(1024)}) %all-reduce.6.cloned.1.call-update) | async-done | bytes 524304
  90.3 1.5 %dynamic-slice.1 = f32[16384]{0:T(1024)} dynamic-slice(f32[131072]{0:T(1024)} %all-reduce.6.cloned.1.call-done, u32[]{:T(128)S(6)} %multiply.2), dynamic_slice_sizes={16384} | dynamic-slice | bytes 131076
  91.8 0.1 broadcast_in_dim.47
  91.8 0.1 broadcast_in_dim.46
  91.9 9.1 %while.13 = (s32[]{:T(128)}, bf16[4,64,8,128]{3,2,1,0:T(8,128)(2,1)S(1)}, s32[4]{0:T(128)S(1)}, bf16[320,8,128]{2,0,1:T(8,128)(2,1)S(1)}, s32[]{:T(128)}, /*inde...) while((s32[]{:T(128)}, ...), condition=%wide.region_3.4_spmd, body=%wide.region_0.3_spmd.sunk | while | flops 34038152 | bytes 1859840 | solution.py:57
  92.0 0.6 dynamic_slice.47
  93.2 0.1 compare_and_fusion.2
  93.4 0.5 fusion.37
  93.8 0.3 fusion.38
  94.1 0.1 copy_dynamic-update-slice_fusion.2
  94.2 0.6 dynamic_slice.47
  95.5 0.1 compare_and_fusion.2
  95.6 0.5 fusion.37
  96.1 0.3 fusion.38
  96.4 0.1 copy_dynamic-update-slice_fusion.2
  96.5 0.6 dynamic_slice.47
  97.8 0.1 compare_and_fusion.2
  97.9 0.5 fusion.37
  98.4 0.3 fusion.38
  98.6 0.1 copy_dynamic-update-slice_fusion.2
  98.8 0.6 dynamic_slice.47
  100.0 0.1 compare_and_fusion.2
  100.2 0.5 fusion.37
  100.6 0.3 fusion.38
  100.9 0.1 copy_dynamic-update-slice_fusion.2
  101.0 1.0 broadcast_in_dim_reshape.3
  102.0 24.8 %all-reduce.4.cloned.1.call-done = f32[16384]{0:T(1024)} async-done(((f32[16384]{0:T(1024)}), f32[16384]{0:T(1024)}) %all-reduce.4.cloned.1.call-update) | async-done | bytes 65552 | tf_op jit(solution)/shard_map/psum | solution.py:66
  126.8 1.5 %broadcast_multiply_fusion = f32[16384]{0:T(1024)} fusion(f32[16384]{0:T(1024)} %all-reduce.4.cloned.1.call-done), kind=kLoop, calls=%fused_computation.26 | loop fusion | flops 16384 | bytes 131072 | tf_op jit(solution)/shard_map/div | solution.py:67
  (28 shorter events, 0.2 us)
Async XLA Ops:
  9.0 4.4 %copy-start.1 = (bf16[1,128,512]{2,1,0:T(8,128)(2,1)S(1)}, bf16[1,128,512]{2,1,0:T(8,128)(2,1)}, u32[]{:S(2)}) copy-start(bf16[1,128,512]{2,1,0:T(8,128)(2,1)} %param.8) | copy-start | bytes 393220
  9.0 8.9 %all-to-all-start.2 = ((bf16[128,4,128]{2,0,1:T(8,128)(2,1)}), bf16[128,4,128]{2,0,1:T(8,128)(2,1)S(1)}, u32[]{:S(2)}, u32[]{:S(2)}) async-start(bf16[128,4,128]{2,0,1:T(8,128)(2,1)} %copy.39), calls=%async_computation.2 | async-start | bytes 262144 | tf_op jit(solution)/shard_map/all_to_all | solution.py:26
  13.3 9.3 %copy-start = (bf16[1,128,2048]{2,1,0:T(8,128)(2,1)S(1)}, bf16[1,128,2048]{2,1,0:T(8,128)(2,1)}, u32[]{:S(2)}) copy-start(bf16[1,128,2048]{2,1,0:T(8,128)(2,1)} %param.6) | copy-start | bytes 1572868
  17.9 7.8 %all-to-all-start = ((bf16[128,4,128]{2,0,1:T(8,128)(2,1)}), bf16[128,4,128]{2,0,1:T(8,128)(2,1)S(1)}, u32[]{:S(2)}, u32[]{:S(2)}) async-start(bf16[128,4,128]{2,0,1:T(8,128)(2,1)} %copy.32), calls=%async_computation | async-start | bytes 262144 | tf_op jit(solution)/shard_map/all_to_all | solution.py:27
  21.3 13.5 %collective-permute-start.1 = (bf16[64,2,128]{2,0,1:T(8,128)(2,1)S(1)}, bf16[64,2,128]{2,0,1:T(8,128)(2,1)S(1)}, u32[]{:S(2)}, u32[]{:S(2)}) collective-permute-start(bf16[64,2,128]{2,0,1:T(8,128)(2,1)S(1)} %slice.9), channel_id=1, source_target_pairs={{0,2},{2,4},{4,6},{1,3},{3,5},{5,7},{8,10},{10,12},{12,14},{9,11},... | collective-permute-start | bytes 98312 | tf_op jit(solution)/shard_map/ppermute | solution.py:14
  25.7 12.6 %all-to-all-start.1 = ((bf16[128,16,128]{2,0,1:T(8,128)(2,1)}), bf16[128,16,128]{2,0,1:T(8,128)(2,1)S(1)}, u32[]{:S(2)}, u32[]{:S(2)}) async-start(bf16[128,16,128]{2,0,1:T(8,128)(2,1)} %copy.35), calls=%async_computation.1 | async-start | bytes 1048576 | tf_op jit(solution)/shard_map/all_to_all | solution.py:25
  29.2 61.0 %all-reduce.6.cloned.1.call-start = ((), (), s32[]{:S(2)}) async-start(), calls=%async_computation.4 | async-start | bytes 1048576
  30.0 96.8 %all-reduce.4.cloned.1.call-start = ((), (), s32[]{:S(2)}) async-start(), calls=%async_computation.3 | async-start | bytes 131072 | tf_op jit(solution)/shard_map/psum | solution.py:66
  30.0 0.7 copy-start.2
  32.0 3.7 %collective-permute-start = (bf16[64,2,128]{2,0,1:T(8,128)(2,1)S(1)}, bf16[64,2,128]{2,0,1:T(8,128)(2,1)S(1)}, u32[]{:S(2)}, u32[]{:S(2)}) collective-permute-start(bf16[64,2,128]{2,0,1:T(8,128)(2,1)S(1)} %slice.8), channel_id=1, source_target_pairs={{0,2},{2,4},{4,6},{1,3},{3,5},{5,7},{8,10},{10,12},{12,14},{9,11},... | collective-permute-start | bytes 98312 | tf_op jit(solution)/shard_map/ppermute | solution.py:14
Sparse Core Ops, SparseCore 0:
  33.1 57.0 all-reduce.5
  93.1 33.6 all-reduce.3
where the time goes:
time: 136 us; the launch traced here: 135 us
  waiting for transfers between devices  86 us (63%)
  starting transfers between devices  15.5 us (11%)
  between operations  14.9 us (11%)
  local copies, waits for them, and re-layouts  11.1 us (8%)
  loops' own time  2.97 us (2%)
  matrix products  2.88 us (2%)
  other arithmetic  1.87 us (1%)
    unnamed x3, waiting for transfers between devices  52.3 us
    psum x1, waiting for transfers between devices, average(): total = lax.psum(share, 'dp')  24.8 us
    all_to_all x1, starting transfers between devices, attend(): lax.all_to_all(k_heads, 'aa', split_axis=1, concat_axis=0, tiled=True)  4.37 us
    ppermute x2, starting transfers between devices, shifted(): return lax.ppermute(value, axis, pairs)  4.15 us
    unnamed x11, local copies, waits for them, and re-layouts  4.12 us
    all_to_all x1, waiting for transfers between devices, attend(): lax.all_to_all(k_heads, 'aa', split_axis=1, concat_axis=0, tiled=True)  3.66 us
    all_to_all x1, starting transfers between devices, attend(): lax.all_to_all(q_heads, 'aa', split_axis=1, concat_axis=0, tiled=True)  3.49 us
    all_to_all x1, starting transfers between devices, attend(): lax.all_to_all(v_heads, 'aa', split_axis=1, concat_axis=0, tiled=True)  3.38 us
  transfers between devices with their start and end apart: 7, of which 6 were waited for; matrix products, arithmetic and copies ran while one was open for 8% of the time, Pallas kernels for 0%

commit v1 on v0

--- a/solution.py
+++ b/solution.py
@@ -63,7 +63,7 @@
     replicas = lax.axis_size("dp")
     flat_grad = grad_parts.reshape(-1)
     share = lax.psum_scatter(flat_grad, ("blk", "aa"), scatter_dimension=0, tiled=True)
-    total = lax.psum(share, "dp")
+    total = jnp.sum(lax.all_gather(share, "dp"), axis=0)
     return total / (members * replicas)
 
 

time: 136 us -> 113 us (0.83)
  waiting for transfers between devices: 86 us -> 51 us
  blocking collectives: 0 us -> 13.9 us
    psum x1 -> x0, waiting for transfers between devices: 24.8 us -> none  [average(): total = lax.psum(share, 'dp')]
    all_gather x0 -> x1, blocking collectives: none -> 13.9 us  [average(): total = jnp.sum(lax.all_gather(share, 'dp'), axis=0)]
    unnamed x3 -> x2, waiting for transfers between devices: 52.3 us -> 42 us
    unnamed x11 -> x12, local copies, waits for them, and re-layouts: 4.12 us -> 3.51 us
  transfers between devices with their start and end apart: 7 -> 6, of which waited for: 6 -> 5; matrix products, arithmetic and copies ran while one was open for 8% -> 9% of each run, Pallas kernels for 0% -> 0%
where the time goes in v1:
time: 113 us
  waiting for transfers between devices  51 us (45%)
  starting transfers between devices  15.4 us (14%)
  between operations  14.9 us (13%)
  blocking collectives  13.9 us (12%)
  local copies, waits for them, and re-layouts  10.6 us (9%)
  loops' own time  2.97 us (3%)
  matrix products  2.87 us (3%)
  other arithmetic  1.19 us (1%)
    unnamed x2, waiting for transfers between devices  42 us
    all_gather x1, blocking collectives, average(): total = jnp.sum(lax.all_gather(share, 'dp'), axis=0)  13.9 us
    all_to_all x1, starting transfers between devices, attend(): lax.all_to_all(k_heads, 'aa', split_axis=1, concat_axis=0, tiled=True)  4.37 us
    ppermute x2, starting transfers between devices, shifted(): return lax.ppermute(value, axis, pairs)  4.15 us
    all_to_all x1, waiting for transfers between devices, attend(): lax.all_to_all(k_heads, 'aa', split_axis=1, concat_axis=0, tiled=True)  3.66 us
    unnamed x12, local copies, waits for them, and re-layouts  3.51 us
    all_to_all x1, starting transfers between devices, attend(): lax.all_to_all(q_heads, 'aa', split_axis=1, concat_axis=0, tiled=True)  3.49 us
    all_to_all x1, starting transfers between devices, attend(): lax.all_to_all(v_heads, 'aa', split_axis=1, concat_axis=0, tiled=True)  3.38 us
  transfers between devices with their start and end apart: 6, of which 5 were waited for; matrix products, arithmetic and copies ran while one was open for 9% of the time, Pallas kernels for 0%

profile of v1, /device:TPU:0, one launch (start us, length us, event | category | flops | bytes accessed | tf_op | source)
XLA Modules:
  0.0 112.8 jit_solution(17556771901272356881)
XLA Ops:
  7.2 1.0 copy.50
  8.2 0.8 copy.51
  9.0 4.4 %all-to-all-start.2 = ((bf16[128,4,128]{2,0,1:T(8,128)(2,1)}), bf16[128,4,128]{2,0,1:T(8,128)(2,1)S(1)}, u32[]{:S(2)}, u32[]{:S(2)}) async-start(bf16[128,4,128]{2,0,1:T(8,128)(2,1)} %copy.51), calls=%async_computation.2 | async-start | bytes 262144 | tf_op jit(solution)/shard_map/all_to_all | solution.py:26
  13.3 0.1 copy.43
  13.5 0.8 copy.44
  14.2 3.7 %all-to-all-done.2 = bf16[128,4,128]{2,0,1:T(8,128)(2,1)S(1)} async-done(((bf16[128,4,128]{2,0,1:T(8,128)(2,1)}), bf16[128,4,128]{2,0,1:T(8,128)(2,1)S(1)}, u32[]{:S(2)}, u32[]{:S(2)}) %all-to-all-start.2) | async-done | bytes 131104 | tf_op jit(solution)/shard_map/all_to_all | solution.py:26
  17.9 3.4 %all-to-all-start = ((bf16[128,4,128]{2,0,1:T(8,128)(2,1)}), bf16[128,4,128]{2,0,1:T(8,128)(2,1)S(1)}, u32[]{:S(2)}, u32[]{:S(2)}) async-start(bf16[128,4,128]{2,0,1:T(8,128)(2,1)} %copy.44), calls=%async_computation | async-start | bytes 262144 | tf_op jit(solution)/shard_map/all_to_all | solution.py:27
  21.3 1.3 %collective-permute-start.1 = (bf16[64,2,128]{2,0,1:T(8,128)(2,1)S(1)}, bf16[64,2,128]{2,0,1:T(8,128)(2,1)S(1)}, u32[]{:S(2)}, u32[]{:S(2)}) collective-permute-start(bf16[64,2,128]{2,0,1:T(8,128)(2,1)S(1)} %slice.9), channel_id=1, source_target_pairs={{0,2},{2,4},{4,6},{1,3},{3,5},{5,7},{8,10},{10,12},{12,14},{9,11},... | collective-permute-start | bytes 98312 | tf_op jit(solution)/shard_map/ppermute | solution.py:14
  22.6 0.3 copy.46
  22.9 1.0 copy.47
  23.9 1.8 %all-to-all-done = bf16[128,4,128]{2,0,1:T(8,128)(2,1)S(1)} async-done(((bf16[128,4,128]{2,0,1:T(8,128)(2,1)}), bf16[128,4,128]{2,0,1:T(8,128)(2,1)S(1)}, u32[]{:S(2)}, u32[]{:S(2)}) %all-to-all-start) | async-done | bytes 131104 | tf_op jit(solution)/shard_map/all_to_all | solution.py:27
  25.7 3.5 %all-to-all-start.1 = ((bf16[128,16,128]{2,0,1:T(8,128)(2,1)}), bf16[128,16,128]{2,0,1:T(8,128)(2,1)S(1)}, u32[]{:S(2)}, u32[]{:S(2)}) async-start(bf16[128,16,128]{2,0,1:T(8,128)(2,1)} %copy.47), calls=%async_computation.1 | async-start | bytes 1048576 | tf_op jit(solution)/shard_map/all_to_all | solution.py:25
  29.3 0.7 all-reduce.3.cloned.1.call-update
  30.0 0.6 copy-done.2
  30.6 0.6 dynamic-slice
  31.9 2.9 %collective-permute-start = (bf16[64,2,128]{2,0,1:T(8,128)(2,1)S(1)}, bf16[64,2,128]{2,0,1:T(8,128)(2,1)S(1)}, u32[]{:S(2)}, u32[]{:S(2)}) collective-permute-start(bf16[64,2,128]{2,0,1:T(8,128)(2,1)S(1)} %slice.8), channel_id=1, source_target_pairs={{0,2},{2,4},{4,6},{1,3},{3,5},{5,7},{8,10},{10,12},{12,14},{9,11},... | collective-permute-start | bytes 98312 | tf_op jit(solution)/shard_map/ppermute | solution.py:14
  34.8 0.8 collective-permute-done
  35.7 2.7 %all-to-all-done.1 = bf16[128,16,128]{2,0,1:T(8,128)(2,1)S(1)} async-done(((bf16[128,16,128]{2,0,1:T(8,128)(2,1)}), bf16[128,16,128]{2,0,1:T(8,128)(2,1)S(1)}, u32[]{:S(2)}, u32[]{:S(2)}) %all-to-all-start.1) | async-done | bytes 524320 | tf_op jit(solution)/shard_map/all_to_all | solution.py:25
  38.4 0.3 copy.49
  38.7 0.1 broadcast_in_dim.47
  38.8 0.1 broadcast_in_dim.46
  38.9 9.0 %while.13 = (s32[]{:T(128)}, bf16[4,64,8,128]{3,2,1,0:T(8,128)(2,1)S(1)}, s32[4]{0:T(128)S(1)}, bf16[320,8,128]{2,0,1:T(8,128)(2,1)S(1)}, s32[]{:T(128)}, /*inde...) while((s32[]{:T(128)}, ...), condition=%wide.region_3.4_spmd, body=%wide.region_0.3_spmd.sunk | while | flops 34038152 | bytes 1859840 | solution.py:57
  38.9 0.6 dynamic_slice.47
  40.2 0.1 compare_and_fusion.2
  40.3 0.5 fusion.37
  40.8 0.3 fusion.38
  41.0 0.1 copy_dynamic-update-slice_fusion.2
  41.2 0.6 dynamic_slice.47
  42.4 0.1 compare_and_fusion.2
  42.6 0.5 fusion.37
  43.0 0.3 fusion.38
  43.3 0.1 copy_dynamic-update-slice_fusion.2
  43.4 0.6 dynamic_slice.47
  44.7 0.1 compare_and_fusion.2
  44.8 0.5 fusion.37
  45.3 0.3 fusion.38
  45.6 0.1 copy_dynamic-update-slice_fusion.2
  45.7 0.6 dynamic_slice.47
  47.1 0.5 fusion.37
  47.5 0.3 fusion.38
  47.8 0.1 copy_dynamic-update-slice_fusion.2
  47.9 1.0 broadcast_in_dim_reshape.3
  49.0 41.3 %all-reduce.3.cloned.1.call-done = f32[131072]{0:T(1024)} async-done(((f32[131072]{0:T(1024)}), f32[131072]{0:T(1024)}) %all-reduce.3.cloned.1.call-update) | async-done | bytes 524304
  90.3 0.8 dynamic-slice-done
  91.1 13.9 %all-gather = f32[65536]{0:T(1024)S(1)} all-gather(f32[16384]{0:T(1024)S(1)} %dynamic-slice-done), channel_id=2, replica_groups=mesh['dp'=4,'blk'=4,'aa'=2] {'dp'}, dimensions={0}, use_global_device_ids=true | all-gather | bytes 327680 | tf_op jit(solution)/shard_map/all_gather | solution.py:66
  105.0 0.1 reshape.91
  105.1 0.2 reduce_sum.22
  105.3 0.6 broadcast_multiply_fusion
  (29 shorter events, 0.3 us)
Async XLA Ops:
  9.0 4.4 %copy-start.1 = (bf16[1,128,512]{2,1,0:T(8,128)(2,1)S(1)}, bf16[1,128,512]{2,1,0:T(8,128)(2,1)}, u32[]{:S(2)}) copy-start(bf16[1,128,512]{2,1,0:T(8,128)(2,1)} %param.8) | copy-start | bytes 393220
  9.0 8.9 %all-to-all-start.2 = ((bf16[128,4,128]{2,0,1:T(8,128)(2,1)}), bf16[128,4,128]{2,0,1:T(8,128)(2,1)S(1)}, u32[]{:S(2)}, u32[]{:S(2)}) async-start(bf16[128,4,128]{2,0,1:T(8,128)(2,1)} %copy.51), calls=%async_computation.2 | async-start | bytes 262144 | tf_op jit(solution)/shard_map/all_to_all | solution.py:26
  13.3 9.3 %copy-start = (bf16[1,128,2048]{2,1,0:T(8,128)(2,1)S(1)}, bf16[1,128,2048]{2,1,0:T(8,128)(2,1)}, u32[]{:S(2)}) copy-start(bf16[1,128,2048]{2,1,0:T(8,128)(2,1)} %param.6) | copy-start | bytes 1572868
  17.9 7.8 %all-to-all-start = ((bf16[128,4,128]{2,0,1:T(8,128)(2,1)}), bf16[128,4,128]{2,0,1:T(8,128)(2,1)S(1)}, u32[]{:S(2)}, u32[]{:S(2)}) async-start(bf16[128,4,128]{2,0,1:T(8,128)(2,1)} %copy.44), calls=%async_computation | async-start | bytes 262144 | tf_op jit(solution)/shard_map/all_to_all | solution.py:27
  21.3 13.5 %collective-permute-start.1 = (bf16[64,2,128]{2,0,1:T(8,128)(2,1)S(1)}, bf16[64,2,128]{2,0,1:T(8,128)(2,1)S(1)}, u32[]{:S(2)}, u32[]{:S(2)}) collective-permute-start(bf16[64,2,128]{2,0,1:T(8,128)(2,1)S(1)} %slice.9), channel_id=1, source_target_pairs={{0,2},{2,4},{4,6},{1,3},{3,5},{5,7},{8,10},{10,12},{12,14},{9,11},... | collective-permute-start | bytes 98312 | tf_op jit(solution)/shard_map/ppermute | solution.py:14
  25.7 12.6 %all-to-all-start.1 = ((bf16[128,16,128]{2,0,1:T(8,128)(2,1)}), bf16[128,16,128]{2,0,1:T(8,128)(2,1)S(1)}, u32[]{:S(2)}, u32[]{:S(2)}) async-start(bf16[128,16,128]{2,0,1:T(8,128)(2,1)} %copy.47), calls=%async_computation.1 | async-start | bytes 1048576 | tf_op jit(solution)/shard_map/all_to_all | solution.py:25
  29.2 61.0 %all-reduce.3.cloned.1.call-start = ((), (), s32[]{:S(2)}) async-start(), calls=%async_computation.3 | async-start | bytes 1048576
  30.0 0.7 copy-start.2
  31.9 3.7 %collective-permute-start = (bf16[64,2,128]{2,0,1:T(8,128)(2,1)S(1)}, bf16[64,2,128]{2,0,1:T(8,128)(2,1)S(1)}, u32[]{:S(2)}, u32[]{:S(2)}) collective-permute-start(bf16[64,2,128]{2,0,1:T(8,128)(2,1)S(1)} %slice.8), channel_id=1, source_target_pairs={{0,2},{2,4},{4,6},{1,3},{3,5},{5,7},{8,10},{10,12},{12,14},{9,11},... | collective-permute-start | bytes 98312 | tf_op jit(solution)/shard_map/ppermute | solution.py:14
  90.3 0.8 dynamic-slice-start
Sparse Core Ops, SparseCore 0:
  33.1 57.0 all-reduce.2
